TPU v7x, 32 devices: a whole 2x2x4 slice. The times are simulated.
32 devices in a mesh: groups: 2 (over y), range: 8 (over z, x), sub: 2 (over core).
Axes of the slice: x: 2, y: 2, z: 4, core: 2. Of those that a mesh axis runs over, the one named last changes fastest.
Arguments:
- samples: float32 [2, 1024, 32, 128], P(None, ('groups', 'range', 'sub')), parts along dimension 1, may hold values from -6 to 6
- beam_weights: float32 [32, 8, 2, 64, 128], P(('groups', 'range'), None, None, None, 'sub'), parts along dimension 0, may hold values from -0.25 to 0.25
- subarrays: int32 [32, 8, 64], P(('groups', 'range', 'sub')), parts along dimension 0, may hold values from 0 to 511, as said below
- training: int32 [64], P(('groups', 'range', 'sub')), parts along dimension 0, may hold values 0 or 1
Outputs:
- covariance: float32 [32, 8, 64, 128], P(('groups', 'range', 'sub')), parts along dimension 0
- filtered: float32 [2, 128, 64, 128], P(None, None, ('groups', 'range', 'sub')), parts along dimension 2
- energy: float32 [256], P('groups'), parts along dimension 0
There are 2 independent parts, one for each index of `groups`. A program takes and returns all parts, laid end to end along the dimension named above; each array names one. Nothing has to cross between parts.
Inputs may be any that keep to these rules, and one draw needn't show every extreme that they name: `subarrays`: in each gate block the 512 indices are all 512 channels, each once.
All inputs are finite; a program needn't handle non-finite values. No bound on the sum of `training` on one device may be relied on, other than what follows from the above.
Results may differ from a plain program's by a relative error of at most 0.0003.
Values sent between devices are 32-bit elements; how exact they have to be, the bound alone decides.
No kernel may reach another device: no remote copies, remote signals or barrier semaphores. Data moves between devices by JAX's collectives and lax.ppermute only.
A program may use at most 64 MiB of HBM per device.

v0:
```python
import jax
import jax.numpy as jnp
from jax import lax
from jax.sharding import PartitionSpec as P

GB = 2


loading = 0.05


def block_terms(snaps, chosen, weights, masked, factor):
    highest = lax.Precision.HIGHEST
    picked = jnp.take(snaps, chosen, axis=1)
    real_part = picked[0]
    imag_part = picked[1]
    real_masked = real_part * masked
    imag_masked = imag_part * masked
    cov_real = (
        jnp.einsum("snx,smx->snm", real_masked, real_part, precision=highest)
        + jnp.einsum("snx,smx->snm", imag_masked, imag_part, precision=highest)
    ) * factor
    cov_imag = (
        jnp.einsum("snx,smx->snm", imag_masked, real_part, precision=highest)
        - jnp.einsum("snx,smx->snm", real_masked, imag_part, precision=highest)
    ) * factor
    w_real = weights[:, 0]
    w_imag = weights[:, 1]
    out_real = jnp.einsum("snk,snx->kx", w_real, real_part, precision=highest) + jnp.einsum(
        "snk,snx->kx", w_imag, imag_part, precision=highest
    )
    out_imag = jnp.einsum("snk,snx->kx", w_real, imag_part, precision=highest) - jnp.einsum(
        "snk,snx->kx", w_imag, real_part, precision=highest
    )
    prod_real = jnp.einsum("snm,smk->snk", cov_real, w_real, precision=highest) - jnp.einsum(
        "snm,smk->snk", cov_imag, w_imag, precision=highest
    )
    prod_imag = jnp.einsum("snm,smk->snk", cov_real, w_imag, precision=highest) + jnp.einsum(
        "snm,smk->snk", cov_imag, w_real, precision=highest
    )
    quadratic = jnp.sum(w_real * prod_real + w_imag * prod_imag, axis=(0, 1))
    inverse = 1.0 / jnp.sqrt(quadratic + loading)
    filtered = jnp.stack([out_real * inverse[:, None], out_imag * inverse[:, None]])
    energy = jnp.sum(out_real * out_real + out_imag * out_imag, axis=1)
    covariance = jnp.concatenate([cov_real, cov_imag], axis=-1)
    return (covariance, filtered, energy)


def body(samples, beam_weights, subarrays, training):
    range_count = lax.axis_size("range")
    core_count = lax.axis_size("sub")
    parts_iq, chan_dev, all_gates, pulses = samples.shape
    gate_dev = all_gates // (range_count * core_count)
    channels = chan_dev * range_count * core_count
    blocks_dev = gate_dev // GB
    spread = samples.reshape(parts_iq, 1, 1, chan_dev, range_count, core_count, gate_dev, pulses)
    turned = lax.all_to_all(
        lax.all_to_all(spread, "range", split_axis=4, concat_axis=1, tiled=True),
        "sub",
        split_axis=5,
        concat_axis=2,
        tiled=True,
    )
    local_data = turned.reshape(parts_iq, channels, blocks_dev, GB * pulses).transpose(2, 0, 1, 3)
    mine = lax.all_to_all(beam_weights, "sub", split_axis=0, concat_axis=4, tiled=True)
    gates_on = training.astype(jnp.float32).reshape(blocks_dev, GB)
    masked = jnp.repeat(gates_on, pulses, axis=1)
    factor = 1.0 / (GB * pulses)
    covs, filts, energies = jax.vmap(block_terms, in_axes=(0, 0, 0, 0, None))(
        local_data, subarrays, mine, masked, factor
    )
    beams = filts.shape[2]
    filtered = filts.reshape(blocks_dev, parts_iq, beams, GB, pulses).transpose(1, 2, 0, 3, 4)
    filtered = filtered.reshape(parts_iq, beams, gate_dev, pulses)
    total = lax.psum(jnp.sum(energies, axis=0), ("range", "sub"))
    energy = total / (all_gates * pulses)
    return (covs, filtered, energy)


def solution(mesh):
    placed = (
        P(None, ("groups", "range", "sub"), None, None),
        P(("groups", "range"), None, None, None, "sub"),
        P(("groups", "range", "sub"), None, None),
        P(("groups", "range", "sub")),
    )
    return jax.shard_map(
        body,
        mesh=mesh,
        in_specs=placed,
        out_specs=(
            P(("groups", "range", "sub"), None, None, None),
            P(None, None, ("groups", "range", "sub"), None),
            P("groups"),
        ),
        check_vma=False,
    )
```

profile of v0, /device:TPU:0, one launch (start us, length us, event | category | flops | bytes accessed | tf_op | source)
XLA Modules:
  0.0 92.5 jit_solution(9004139148378862796)
XLA Ops:
  0.6 2.5 %reshape.157 = f32[2,1,65536]{2,1,0:T(1,128)} reshape(f32[2,8,2,64,64]{4,3,2,1,0:T(8,128)} %param.5) | data formatting | bytes 1048576
  3.2 3.5 %all-to-all-start.2 = ((f32[2,1,65536]{2,1,0:T(1,128)}), f32[2,1,65536]{2,1,0:T(1,128)S(1)}, u32[]{:S(2)}, u32[]{:S(2)}) async-start(f32[2,1,65536]{2,1,0:T(1,128)} %reshape.157), calls=%async_computation.2 | async-start | bytes 1048576 | tf_op jit(solution)/shard_map/all_to_all | solution.py:65
  6.7 1.6 %copy.24 = f32[2,1,1,32,8,2,2,128]{7,6,3,5,0,2,1,4:T(2,128)} copy(f32[2,1,1,32,8,2,2,128]{7,6,5,4,3,0,2,1:T(2,128)S(1)} %bitcast.103) | data formatting | bytes 2097152 | tf_op jit(solution)/shard_map/reshape | solution.py:56
  8.4 7.4 %all-to-all-start = ((f32[2,1,1,32,8,2,2,128]{7,6,3,5,0,2,1,4:T(2,128)}), f32[2,1,1,32,8,2,2,128]{7,6,3,5,0,2,1,4:T(2,128)S(1)}, u32[]{:S(2)}, u32[]{:S(2)}) async-start(f32[2,1,1,32,8,2,2,128]{7,6,3,5,0,2,1,4:T(2,128)} %copy.24), calls=%async_computation | async-start | bytes 2097152 | tf_op jit(solution)/shard_map/all_to_all | solution.py:58
  16.4 2.3 %reduce.5 = f32[2,65536]{1,0:T(2,128)S(1)} reduce(f32[2,1,65536]{2,1,0:T(1,128)S(1)} %all-to-all-done.2, f32[]{:T(128)} %broadcast.75), dimensions={1}, to_apply=%all_to_all.44.reduce_sub_computation | reduce | bytes 1048580 | tf_op jit(solution)/shard_map/all_to_all | solution.py:65
  18.8 0.6 reshape.158
  19.4 1.9 %copy.29 = f32[1,8,2,64,2,64]{5,4,3,1,2,0:T(2,128)} copy(f32[1,8,2,64,2,64]{5,3,2,1,4,0:T(8,128)S(1)} %bitcast.98) | data formatting | bytes 1048576 | tf_op jit(solution)/shard_map/all_to_all | solution.py:65
  21.2 1.8 %all_to_all.47 = f32[1,8,2,64,128]{4,3,1,2,0:T(8,128)S(1)} reshape(f32[1,8,2,64,2,64]{5,4,3,1,2,0:T(2,128)} %copy.29) | data formatting | bytes 1048576 | tf_op jit(solution)/shard_map/all_to_all | solution.py:65
  23.1 18.9 %all-to-all-done = f32[2,1,1,32,8,2,2,128]{7,6,3,5,0,2,1,4:T(2,128)S(1)} async-done(((f32[2,1,1,32,8,2,2,128]{7,6,3,5,0,2,1,4:T(2,128)}), f32[2,1,1,32,8,2,2,128]{7,6,3,5,0,2,1,4:T(2,128)S(1)}, u32[]{:S(2)}, u32[]{:S(2)}) %all-to-all-start) | async-done | bytes 1048608 | tf_op jit(solution)/shard_map/all_to_all | solution.py:58
  42.1 4.6 %all_to_all.51 = f32[2,8,1,32,1,2,2,128]{7,6,3,1,0,4,2,5:T(2,128)S(1)} all-to-all(f32[2,8,1,32,1,2,2,128]{7,6,3,1,0,4,2,5:T(2,128)S(1)} %copy.25), channel_id=1, replica_groups=mesh['groups'=2,'range'=8,'sub'=2] {'sub'}, dimensions={5} | all-to-all | bytes 2097152 | tf_op jit(solution)/shard_map/all_to_all | solution.py:57
  46.8 0.8 copy.27
  47.6 2.3 %gather_fusion = f32[512,2,256]{2,1,0:T(2,128)S(1)} fusion(f32[1,2,512,256]{3,1,2,0:T(2,128)S(1)} %copy.27, s32[512]{0:T(512)S(1)} %reshape.147), kind=kCustom, calls=%fused_computation | custom fusion | bytes 2101248 | tf_op jit(solution)/shard_map/vmap(jit(_take))/gather | solution.py:14
  50.2 1.0 %convolution_bitcast_fusion.2 = f32[256,128]{1,0:T(8,128)S(1)} fusion(f32[1,2,8,64,256]{4,3,2,1,0:T(8,128)S(1)} %broadcast_select_fusion, f32[1,8,2,64,128]{4,3,1,2,0:T(8,128)S(1)} %all_to_all.47), kind=kOutput, calls=%fused_computation.13 | convolution fusion | flops 201326592 | bytes 917504 | tf_op jit(solution)/shard_map/vmap(snk,snx->kx)/dot_general | solution.py:29
  51.2 1.0 %convolution_bitcast_fusion = f32[256,128]{1,0:T(8,128)S(1)} fusion(f32[1,2,8,64,256]{4,3,2,1,0:T(8,128)S(1)} %broadcast_select_fusion, f32[1,8,2,64,128]{4,3,1,2,0:T(8,128)S(1)} %all_to_all.47), kind=kOutput, calls=%fused_computation.11 | convolution fusion | flops 201326592 | bytes 917504 | tf_op jit(solution)/shard_map/vmap(snk,snx->kx)/dot_general | solution.py:32
  52.2 0.6 fusion.12
  52.8 0.6 fusion.2
  54.3 0.6 fusion.8
  54.9 1.0 %fusion.6 = f32[256,128]{1,0:T(8,128)S(1)} fusion(f32[256,128]{1,0:T(8,128)S(1)} %convolution_bitcast_fusion.2, f32[1,2,8,64,256]{4,3,2,1,0:T(8,128)S(1)} %broadcast_select_fusion, f32[1,8,2,64,128]{4,3,1,2,0:T(8,128)S(1)} %all_to_all.47), kind=kOutput, calls=%fused_computation.15 | convolution fusion | flops 201359360 | bytes 1048576 | tf_op jit(solution)/shard_map/vmap(snk,snx->kx)/dot_general | solution.py:29
  55.9 0.6 fusion.3
  57.4 1.0 %add_reduce_fusion = (f32[128]{0:T(128)S(1)}, f32[256,128]{1,0:T(8,128)S(1)}, f32[256,128]{1,0:T(8,128)S(1)}) fusion(f32[256,128]{1,0:T(8,128)S(1)} %fusion.6, f32[128]{0:T(128)S(1)} %add_rsqrt_fusion, f32[256,128]{1,0:T(8,128)S(1)} %convolution_bitcast_fusion, f32[1,8,2,64,128]{4,3,1,2,0:T(8,128)S(1)} %all_to_all.47, ...), kind=kOutput, calls=%fused_computation.36 | convolution fusion | flops 201555840 | bytes 1311744 | tf_op jit(solution)/shard_map/vmap(snk,snx->kx)/dot_general | solution.py:32
  58.4 31.6 %psum.7 = f32[128]{0:T(128)S(1)} all-reduce(f32[128]{0:T(128)S(1)} %get-tuple-element.3), channel_id=1, replica_groups=mesh['groups'=2,'range'=8,'sub'=2] {'range','sub'}, use_global_device_ids=true, to_apply=%region_2.3 | all-reduce | flops 128 | bytes 1024 | tf_op jit(solution)/shard_map/psum | solution.py:75
  90.1 0.5 broadcast_multiply_fusion.2
  90.8 0.8 pad_maximum_fusion
  91.7 0.8 pad_maximum_fusion.1
  (26 shorter events, 3.1 us)
Async XLA Ops:
  0.6 6.0 %copy-start = (f32[2,32,32,128]{3,2,1,0:T(8,128)S(1)}, f32[2,32,32,128]{3,2,1,0:T(8,128)}, u32[]{:S(2)}) copy-start(f32[2,32,32,128]{3,2,1,0:T(8,128)} %param.4) | copy-start | bytes 3145732
  3.2 5.2 %all-to-all-start.2 = ((f32[2,1,65536]{2,1,0:T(1,128)}), f32[2,1,65536]{2,1,0:T(1,128)S(1)}, u32[]{:S(2)}, u32[]{:S(2)}) async-start(f32[2,1,65536]{2,1,0:T(1,128)} %reshape.157), calls=%async_computation.2 | async-start | bytes 1048576 | tf_op jit(solution)/shard_map/all_to_all | solution.py:65
  8.2 7.6 %copy-start.2 = (s32[2]{0:T(128)S(1)}, s32[2]{0:T(128)}, u32[]{:S(2)}) copy-start(s32[2]{0:T(128)} %param.7) | copy-start | bytes 28
  8.4 7.4 %copy-start.1 = (s32[1,8,64]{2,1,0:T(8,128)S(1)}, s32[1,8,64]{2,1,0:T(8,128)}, u32[]{:S(2)}) copy-start(s32[1,8,64]{2,1,0:T(8,128)} %param.6) | copy-start | bytes 6148
  8.4 33.7 %all-to-all-start = ((f32[2,1,1,32,8,2,2,128]{7,6,3,5,0,2,1,4:T(2,128)}), f32[2,1,1,32,8,2,2,128]{7,6,3,5,0,2,1,4:T(2,128)S(1)}, u32[]{:S(2)}, u32[]{:S(2)}) async-start(f32[2,1,1,32,8,2,2,128]{7,6,3,5,0,2,1,4:T(2,128)} %copy.24), calls=%async_computation | async-start | bytes 2097152 | tf_op jit(solution)/shard_map/all_to_all | solution.py:58
where the time goes:
time: 92.9 us; the launch traced here: 92.5 us
  blocking collectives  36.2 us (39%)
  waiting for transfers between devices  19.1 us (21%)
  local copies, waits for them, and re-layouts  12.7 us (14%)
  starting transfers between devices  10.9 us (12%)
  matrix products  8.12 us (9%)
  other arithmetic  4.67 us (5%)
    psum x1, blocking collectives, body(): total = lax.psum(jnp.sum(energies, axis=0), ('range', 'sub'))  31.6 us
    all_to_all x1, waiting for transfers between devices, body(): lax.all_to_all(spread, 'range', split_axis=4, concat_axis=1, tiled=True)  18.9 us
    all_to_all x1, starting transfers between devices, body(): lax.all_to_all(spread, 'range', split_axis=4, concat_axis=1, tiled=True)  7.41 us
    all_to_all x1, blocking collectives, body(): lax.all_to_all(lax.all_to_all(spread, 'range', split_axis=4, concat_axis=...  4.58 us
    all_to_all x3, local copies, waits for them, and re-layouts, body(): lax.all_to_all(beam_weights, 'sub', split_axis=0, concat_axis=4, tiled=True)  4.18 us
    all_to_all x1, starting transfers between devices, body(): lax.all_to_all(beam_weights, 'sub', split_axis=0, concat_axis=4, tiled=True)  3.49 us
    unnamed x8, local copies, waits for them, and re-layouts  3.15 us
    gather x4, local copies, waits for them, and re-layouts, block_terms(): picked = jnp.take(snaps, chosen, axis=1)  2.5 us
  transfers between devices with their start and end apart: 2, of which 2 were waited for; matrix products, arithmetic and copies ran while one was open for 8% of the time, Pallas kernels for 0%

commit v1 on v0

v1 whole, which is shorter than its diff:
```python
import functools

import jax
import jax.numpy as jnp
from jax import lax
from jax.experimental import pallas as pl
from jax.experimental.pallas import tpu as pltpu
from jax.sharding import PartitionSpec as P

GB = 2
AXES = ("range", "sub")

loading = 0.05


def split(value):
    high = value.astype(jnp.bfloat16)
    low = (value - high.astype(jnp.float32)).astype(jnp.bfloat16)
    return high, low


def dot(lhs, rhs, dims):
    return lax.dot_general(lhs, rhs, (dims, ((), ())), preferred_element_type=jnp.float32)


def dot3(lhs, rhs, dims):
    (lh, ll), (rh, rl) = lhs, rhs
    return dot(lh, rh, dims) + (dot(lh, rl, dims) + dot(ll, rh, dims))


def local_kernel(core, gates, turned, own, got, chosen, cov_out, filt_out, energy_out, *, factor):
    sources, rows, pulses = turned.shape
    subs, _, size, half = own.shape[1:]
    beams = 2 * half
    chan_dev = rows // (2 * GB)
    channels = sources * chan_dev
    flat = turned.reshape(sources * rows, pulses)

    columns = []
    for iq in range(2):
        for gate in range(GB):
            pieces = [
                flat[pl.ds(src * rows + iq * chan_dev * GB + gate, chan_dev, stride=GB), :]
                for src in range(sources)
            ]
            columns.append(jnp.concatenate(pieces, axis=0))
    snaps = jnp.concatenate(columns, axis=1)
    snap_high, snap_low = split(snaps)
    wanted = chosen[...]
    hot = (wanted == lax.broadcasted_iota(jnp.int32, (subs * size, channels), 1)).astype(jnp.bfloat16)
    rows_of = ((1,), (0,))
    pick_high = dot(hot, snap_high, rows_of).astype(jnp.bfloat16)
    pick_low = dot(hot, snap_low, rows_of).astype(jnp.bfloat16)

    first = core[0] == 0
    mine = own[0]
    other = got[...]
    low_half = jnp.where(first, mine, other)
    high_half = jnp.where(first, other, mine)
    both = jnp.concatenate([low_half, high_half], axis=-1)
    w_real = both[:, 0].reshape(subs * size, beams)
    w_imag = both[:, 1].reshape(subs * size, beams)
    weights = jnp.concatenate([w_real, w_imag], axis=1)
    wt_high, wt_low = split(weights)

    over_rows = ((0,), (0,))
    mixed = dot3((wt_high, wt_low), (pick_high, pick_low), over_rows)
    width = GB * pulses
    out_real = mixed[:beams, :width] + mixed[beams:, width:]
    out_imag = mixed[:beams, width:] - mixed[beams:, :width]
    power = out_real * out_real + out_imag * out_imag
    folded = power[:, :pulses]
    for gate in range(1, GB):
        folded = folded + power[:, gate * pulses:(gate + 1) * pulses]
    total = jnp.sum(folded.T, axis=0, keepdims=True)
    energy_out[...] = jnp.broadcast_to(total, energy_out.shape)

    column_gate = lax.broadcasted_iota(jnp.int32, (1, 2 * width), 1) // pulses % GB
    mask = jnp.zeros((1, 2 * width), jnp.float32)
    for gate in range(GB):
        mask = jnp.where(column_gate == gate, gates[gate].astype(jnp.float32), mask)
    mask = mask.astype(jnp.bfloat16)
    over_cols = ((1,), (1,))
    power_sum = jnp.zeros((size, beams), jnp.float32)
    for s in range(subs):
        part = slice(s * size, (s + 1) * size)
        zh, zl = pick_high[part], pick_low[part]
        right = [
            jnp.concatenate([z, jnp.concatenate([-z[:, width:], z[:, :width]], axis=1)], axis=0)
            for z in (zh, zl)
        ]
        cov = dot3((zh * mask, zl * mask), right, over_cols) * factor
        cov_out[0, s] = cov
        ws_high, ws_low = wt_high[part], wt_low[part]
        stacked = [
            jnp.concatenate([w, jnp.concatenate([-w[:, beams:], w[:, :beams]], axis=1)], axis=0)
            for w in (ws_high, ws_low)
        ]
        prod = dot3(split(cov), stacked, rows_of)
        terms = prod * weights[part]
        power_sum = power_sum + (terms[:, :beams] + terms[:, beams:])
    quadratic = jnp.sum(power_sum, axis=0, keepdims=True)
    inverse = 1.0 / jnp.sqrt(quadratic + loading)
    scale = jnp.broadcast_to(inverse, (pulses, beams)).T
    for iq, value in enumerate((out_real, out_imag)):
        for gate in range(GB):
            filt_out[iq, pl.ds(gate, beams, stride=GB), :] = value[:, gate * pulses:(gate + 1) * pulses] * scale


def body(samples, beam_weights, subarrays, training):
    range_count = lax.axis_size("range")
    core_count = lax.axis_size("sub")
    parts_iq, chan_dev, all_gates, pulses = samples.shape
    devices = range_count * core_count
    gate_dev = all_gates // devices
    subs, _, size, half = beam_weights.shape[1:]
    beams = half * core_count
    channels = chan_dev * devices
    core = lax.axis_index("sub")

    rows = parts_iq * chan_dev * gate_dev
    spread = samples.reshape(parts_iq, chan_dev, devices, gate_dev, pulses).transpose(2, 0, 1, 3, 4)
    spread = spread.reshape(devices, rows, pulses)
    turned = lax.all_to_all(spread, AXES, 0, 0, tiled=True)
    sent = lax.dynamic_index_in_dim(beam_weights, 1 - core, 0, keepdims=False)
    got = lax.ppermute(sent, "sub", [(0, 1), (1, 0)])

    factor = 1.0 / (GB * pulses)
    vmem = pl.BlockSpec(memory_space=pltpu.VMEM)
    whole = lambda shape: pl.BlockSpec(shape, lambda i, core, gates: (0,) * len(shape))
    out_shapes = (
        jax.ShapeDtypeStruct((1, subs, size, 2 * size), jnp.float32),
        jax.ShapeDtypeStruct((parts_iq, beams * gate_dev, pulses), jnp.float32),
        jax.ShapeDtypeStruct((devices, beams), jnp.float32),
    )
    covs, filts, energies = pl.pallas_call(
        functools.partial(local_kernel, factor=factor),
        out_shape=out_shapes,
        grid_spec=pltpu.PrefetchScalarGridSpec(
            num_scalar_prefetch=2,
            grid=(1,),
            in_specs=[
                whole((devices, rows, pulses)),
                pl.BlockSpec((1, subs, 2, size, half), lambda i, core, gates: (core[0], 0, 0, 0, 0)),
                whole((subs, 2, size, half)),
                whole((subs * size, 1)),
            ],
            out_specs=[whole(o.shape) for o in out_shapes],
        ),
    )(core.reshape(1).astype(jnp.int32), training, turned, beam_weights, got, subarrays.reshape(subs * size, 1))
    filtered = filts.reshape(parts_iq, beams, gate_dev, pulses)
    shared = lax.all_to_all(energies, AXES, 0, 0, tiled=True)
    energy = jnp.sum(shared, axis=0) * (1.0 / (all_gates * pulses))
    return (covs, filtered, energy)


def solution(mesh):
    placed = (
        P(None, ("groups", "range", "sub"), None, None),
        P(("groups", "range"), None, None, None, "sub"),
        P(("groups", "range", "sub"), None, None),
        P(("groups", "range", "sub")),
    )
    return jax.shard_map(
        body,
        mesh=mesh,
        in_specs=placed,
        out_specs=(
            P(("groups", "range", "sub"), None, None, None),
            P(None, None, ("groups", "range", "sub"), None),
            P("groups"),
        ),
        check_vma=False,
    )
```

time: 92.9 us -> 55.8 us (0.60)
  blocking collectives: 36.2 us -> 13.2 us
  matrix products: 8.12 us -> 0 us
  local copies, waits for them, and re-layouts: 12.7 us -> 4.86 us
  Pallas kernels: 0 us -> 6.84 us
  other arithmetic: 4.67 us -> 0.55 us
  starting transfers between devices: 10.9 us -> 7.98 us
  waiting for transfers between devices: 19.1 us -> 21.3 us
    psum x1 -> x0, blocking collectives: 31.6 us -> none  [body(): total = lax.psum(jnp.sum(energies, axis=0), ('range', 'sub'))]
    all_to_all x1, blocking collectives: 4.58 us -> 13.2 us  [body(): shared = lax.all_to_all(energies, AXES, 0, 0, tiled=True)]
    dot_general x12 -> x0, matrix products: 8.12 us -> none  [the longest x1 1.02 us: block_terms(): jnp.einsum('snk,snx->kx', w_real, imag_part, precision=highest)]
    pallas_call x0 -> x1, Pallas kernels: none -> 6.84 us  [body(): pl.pallas_call(functools.partial(local_kernel, factor=factor), out_shape=...]
    all_to_all x5 -> x0, local copies, waits for them, and re-layouts: 4.35 us -> none  [the longest x3 4.18 us: body(): lax.all_to_all(beam_weights, 'sub', split_axis=0, concat_axis=4, tiled=True)]
    all_to_all x2 -> x1, starting transfers between devices: 10.9 us -> 7.52 us  [body(): turned = lax.all_to_all(spread, AXES, 0, 0, tiled=True)]
    gather x4 -> x0, local copies, waits for them, and re-layouts: 2.5 us -> none  [block_terms(): picked = jnp.take(snaps, chosen, axis=1)]
    all_to_all x1 -> x0, other arithmetic: 2.32 us -> none  [body(): lax.all_to_all(beam_weights, 'sub', split_axis=0, concat_axis=4, tiled=True)]
  transfers between devices with their start and end apart: 2 -> 2, of which waited for: 2 -> 2; matrix products, arithmetic and copies ran while one was open for 8% -> 2% of each run, Pallas kernels for 0% -> 0%
where the time goes in v1:
time: 55.8 us; the launch traced here: 55.4 us
  waiting for transfers between devices  21.3 us (38%)
  blocking collectives  13.2 us (24%)
  starting transfers between devices  7.98 us (14%)
  Pallas kernels  6.84 us (12%)
  local copies, waits for them, and re-layouts  4.86 us (9%)
  between operations  0.67 us (1%)
    all_to_all x1, waiting for transfers between devices, body(): turned = lax.all_to_all(spread, AXES, 0, 0, tiled=True)  20.8 us
    all_to_all x1, blocking collectives, body(): shared = lax.all_to_all(energies, AXES, 0, 0, tiled=True)  13.2 us
    all_to_all x1, starting transfers between devices, body(): turned = lax.all_to_all(spread, AXES, 0, 0, tiled=True)  7.52 us
    pallas_call x1, Pallas kernels, body(): pl.pallas_call(functools.partial(local_kernel, factor=factor), out_shape=...  6.84 us
    reshape x1, local copies, waits for them, and re-layouts, body(): samples.reshape(parts_iq, chan_dev, devices, gate_dev, pulses)  2.77 us
    unnamed x8, local copies, waits for them, and re-layouts  1.14 us
  transfers between devices with their start and end apart: 2, of which 2 were waited for; matrix products, arithmetic and copies ran while one was open for 2% of the time, Pallas kernels for 0%

profile of v1, /device:TPU:0, one launch (start us, length us, event | category | flops | bytes accessed | tf_op | source)
XLA Modules:
  0.0 55.4 jit_solution(9089761824523693108)
XLA Ops:
  0.6 2.8 %copy.10 = f32[2,32,16,2,128]{4,3,1,0,2:T(2,128)} copy(f32[2,32,16,2,128]{4,3,2,1,0:T(2,128)} %bitcast.11) | data formatting | bytes 2097152 | tf_op jit(solution)/shard_map/reshape | solution.py:122
  3.4 0.0 copy-start.1
  3.4 7.5 %all-to-all-start = ((f32[16,128,128]{2,1,0:T(8,128)}), f32[16,128,128]{2,1,0:T(8,128)S(1)}, u32[]{:S(2)}, u32[]{:S(2)}) async-start(f32[16,128,128]{2,1,0:T(8,128)} %bitcast.3), calls=%async_computation | async-start | bytes 2097152 | tf_op jit(solution)/shard_map/all_to_all | solution.py:124
  10.9 0.0 copy-done.1
  10.9 0.0 copy-start.3
  11.0 0.5 collective-permute-start
  11.5 0.2 copy-done.3
  11.6 0.9 %reshape.28.chosen = s32[512,1]{1,0:T(8,128)} reshape(s32[1,8,64]{2,1,0:T(8,128)S(1)} %copy-done.3) | data formatting | bytes 4096 | tf_op jit(solution)/shard_map/reshape | solution.py:150
  12.5 0.5 collective-permute-done.got
  13.0 0.0 copy-start.2
  13.0 20.8 %all-to-all-done.turned = f32[16,128,128]{2,1,0:T(8,128)S(1)} async-done(((f32[16,128,128]{2,1,0:T(8,128)}), f32[16,128,128]{2,1,0:T(8,128)S(1)}, u32[]{:S(2)}, u32[]{:S(2)}) %all-to-all-start) | async-done | bytes 1048608 | tf_op jit(solution)/shard_map/all_to_all | solution.py:124
  33.8 0.0 copy-start
  33.8 0.0 copy-done.2
  33.8 1.0 %copy-done = f32[16,128,128]{2,1,0:T(8,128)} copy-done((f32[16,128,128]{2,1,0:T(8,128)}, f32[16,128,128]{2,1,0:T(8,128)S(1)}, u32[]{:S(2)}) %copy-start) | copy-done | bytes 1048600
  34.8 6.8 %shard_map.67 = (f32[1,8,64,128]{3,2,1,0:T(8,128)}, f32[2,256,128]{2,1,0:T(8,128)}, f32[16,128]{1,0:T(8,128)}) custom-call(s32[1]{0:T(128)} %bitcast.core, s32[2]{0:T(128)} %gates.1, f32[16,128,128]{2,1,0:T(8,128)} %copy-done, f32[2,8,2,64,64]{4,3,2,1,0:T(8,128)} %own.1, f32[8,2,64,64]{3,2,1,0:T(8,128)} %copy-done.2, s32[512,1]{1,0:T(8,128)} %reshape.28.chosen), custom_call_target="tpu_custom_call" | custom-call | tf_op jit(solution)/shard_map/pallas_call | solution.py:136
  41.6 13.2 %all_to_all.14 = f32[16,1,128]{2,1,0:T(1,128)S(1)} all-to-all(f32[16,1,128]{2,1,0:T(1,128)} %bitcast.12), channel_id=1, replica_groups=mesh['groups'=2,'range'=8,'sub'=2] {'range','sub'}, dimensions={0} | all-to-all | bytes 16384 | tf_op jit(solution)/shard_map/all_to_all | solution.py:152
  54.9 0.5 broadcast_multiply_fusion
  (2 shorter events, 0.1 us)
Async XLA Ops:
  3.4 7.5 %copy-start.1 = (f32[2,8,2,64,64]{4,3,2,1,0:T(8,128)S(1)}, f32[2,8,2,64,64]{4,3,2,1,0:T(8,128)}, u32[]{:S(2)}) copy-start(f32[2,8,2,64,64]{4,3,2,1,0:T(8,128)} %own.1) | copy-start | bytes 1572868
  3.4 30.4 %all-to-all-start = ((f32[16,128,128]{2,1,0:T(8,128)}), f32[16,128,128]{2,1,0:T(8,128)S(1)}, u32[]{:S(2)}, u32[]{:S(2)}) async-start(f32[16,128,128]{2,1,0:T(8,128)} %bitcast.3), calls=%async_computation | async-start | bytes 2097152 | tf_op jit(solution)/shard_map/all_to_all | solution.py:124
  10.9 0.7 %copy-start.3 = (s32[1,8,64]{2,1,0:T(8,128)S(1)}, s32[1,8,64]{2,1,0:T(8,128)}, u32[]{:S(2)}) copy-start(s32[1,8,64]{2,1,0:T(8,128)} %param.6) | copy-start | bytes 6148
  11.0 2.0 %collective-permute-start = (f32[8,2,64,64]{3,2,1,0:T(8,128)S(1)}, f32[8,2,64,64]{3,2,1,0:T(8,128)S(1)}, u32[]{:S(2)}, u32[]{:S(2)}) collective-permute-start(f32[8,2,64,64]{3,2,1,0:T(8,128)S(1)} %dynamic-slice_bitcast_fusion), channel_id=1, source_target_pairs={{0,1},{1,0},{2,3},{3,2},{4,5},{5,4},{6,7},{7,6},{8,9},{9,8},{10,11... | collective-permute-start | bytes 786440 | tf_op jit(solution)/shard_map/ppermute | solution.py:126
  13.0 20.8 %copy-start.2 = (f32[8,2,64,64]{3,2,1,0:T(8,128)}, f32[8,2,64,64]{3,2,1,0:T(8,128)S(1)}, u32[]{:S(2)}) copy-start(f32[8,2,64,64]{3,2,1,0:T(8,128)S(1)} %collective-permute-done.got) | copy-start | bytes 786436
  33.8 1.0 %copy-start = (f32[16,128,128]{2,1,0:T(8,128)}, f32[16,128,128]{2,1,0:T(8,128)S(1)}, u32[]{:S(2)}) copy-start(f32[16,128,128]{2,1,0:T(8,128)S(1)} %all-to-all-done.turned) | copy-start | bytes 3145732

commit v2 on v1

v2 whole, which is shorter than its diff:
```python
import functools

import jax
import jax.numpy as jnp
from jax import lax
from jax.experimental import pallas as pl
from jax.experimental.pallas import tpu as pltpu
from jax.sharding import PartitionSpec as P

GB = 2
AXES = ("range", "sub")
OVER_COLS_ROWS = ((1,), (0,))
OVER_ROWS = ((0,), (0,))
OVER_COLS = ((1,), (1,))

loading = 0.05

VMEM = pl.BlockSpec(memory_space=pltpu.VMEM)
SMEM = pl.BlockSpec(memory_space=pltpu.SMEM)


def split(value):
    high = value.astype(jnp.bfloat16)
    low = (value - high.astype(jnp.float32)).astype(jnp.bfloat16)
    return high, low


def dot(lhs, rhs, dims):
    return lax.dot_general(lhs, rhs, (dims, ((), ())), preferred_element_type=jnp.float32)


def dot3(lhs, rhs, dims):
    (lh, ll), (rh, rl) = lhs, rhs
    return dot(lh, rh, dims) + (dot(lh, rl, dims) + dot(ll, rh, dims))


def spread_kernel(samples, spread):
    parts_iq, chan_step, all_gates, pulses = samples.shape
    devices, rows, _ = spread.shape
    chan_dev = rows // (parts_iq * GB)
    flat = samples.reshape(parts_iq * chan_step * all_gates, pulses)
    start = pl.multiple_of(pl.program_id(0) * chan_step, chan_step)
    for iq in range(parts_iq):
        for gate in range(all_gates):
            dest, inner = divmod(gate, GB)
            row = iq * chan_step * all_gates + gate
            spread[dest, pl.ds((iq * GB + inner) * chan_dev + start, chan_step), :] = flat[
                pl.ds(row, chan_step, stride=all_gates), :
            ]


def prepare_kernel(core, own, got, chosen, hot_out, sub_out, chan_out):
    subs, _, size, half = got.shape
    beams = 2 * half
    channels = hot_out.shape[1]
    wanted = chosen[...]
    hot = (wanted == lax.broadcasted_iota(jnp.int32, (subs * size, channels), 1)).astype(jnp.bfloat16)
    hot_out[...] = hot
    mine = own[core[0]]
    other = got[...]
    first = core[0] == 0
    both = jnp.concatenate([jnp.where(first, mine, other), jnp.where(first, other, mine)], axis=-1)
    weights = jnp.concatenate([both[:, iq].reshape(subs * size, beams) for iq in range(2)], axis=1)
    for index, piece in enumerate(split(weights)):
        sub_out[index] = piece
        chan_out[index] = dot(hot, piece, OVER_ROWS).astype(jnp.bfloat16)


def beam_kernel(turned, weights, snap_out, beam_out, energy_out):
    sources, rows, pulses = turned.shape
    chan_dev = rows // (2 * GB)
    beams = weights.shape[2] // 2
    width = GB * pulses
    columns = [
        turned[:, piece * chan_dev:(piece + 1) * chan_dev, :].reshape(sources * chan_dev, pulses)
        for piece in range(2 * GB)
    ]
    snaps = split(jnp.concatenate(columns, axis=1))
    for index, piece in enumerate(snaps):
        snap_out[index] = piece
    mixed = dot3((weights[0], weights[1]), snaps, OVER_ROWS)
    out_real = mixed[:beams, :width] + mixed[beams:, width:]
    out_imag = mixed[:beams, width:] - mixed[beams:, :width]
    beam_out[0] = out_real
    beam_out[1] = out_imag
    power = out_real * out_real + out_imag * out_imag
    folded = power[:, :pulses]
    for gate in range(1, GB):
        folded = folded + power[:, gate * pulses:(gate + 1) * pulses]
    total = jnp.sum(folded.T, axis=0, keepdims=True)
    energy_out[...] = jnp.broadcast_to(total, energy_out.shape)


def covariance_kernel(gates, hot, snaps, weights, beam_in, cov_out, filt_out, *, factor):
    subs, size = cov_out.shape[1:3]
    beams = weights.shape[2] // 2
    width = beam_in.shape[2]
    pulses = width // GB
    picked = [dot(hot[...], snaps[index], OVER_COLS_ROWS).astype(jnp.bfloat16) for index in range(2)]
    column_gate = lax.broadcasted_iota(jnp.int32, (1, 2 * width), 1) // pulses % GB
    mask = jnp.zeros((1, 2 * width), jnp.float32)
    for gate in range(GB):
        mask = jnp.where(column_gate == gate, gates[gate].astype(jnp.float32), mask)
    mask = mask.astype(jnp.bfloat16)
    power_sum = jnp.zeros((size, beams), jnp.float32)
    for s in range(subs):
        part = slice(s * size, (s + 1) * size)
        rows = [z[part] for z in picked]
        right = [
            jnp.concatenate([z, jnp.concatenate([-z[:, width:], z[:, :width]], axis=1)], axis=0) for z in rows
        ]
        cov = dot3([z * mask for z in rows], right, OVER_COLS) * factor
        cov_out[0, s] = cov
        own = [weights[index, part] for index in range(2)]
        stacked = [
            jnp.concatenate([w, jnp.concatenate([-w[:, beams:], w[:, :beams]], axis=1)], axis=0) for w in own
        ]
        prod = dot3(split(cov), stacked, OVER_COLS_ROWS)
        terms = prod * (own[0].astype(jnp.float32) + own[1].astype(jnp.float32))
        power_sum = power_sum + (terms[:, :beams] + terms[:, beams:])
    quadratic = jnp.sum(power_sum, axis=0, keepdims=True)
    inverse = 1.0 / jnp.sqrt(quadratic + loading)
    scale = jnp.broadcast_to(inverse, (pulses, beams)).T
    for iq in range(2):
        for gate in range(GB):
            filt_out[iq, pl.ds(gate, beams, stride=GB), :] = (
                beam_in[iq, :, gate * pulses:(gate + 1) * pulses] * scale
            )


def near(array):
    return pltpu.with_memory_space_constraint(array, pltpu.VMEM)


def call(kernel, out_shape, in_specs, *operands):
    return pl.pallas_call(
        kernel,
        out_shape=out_shape,
        in_specs=in_specs,
        out_specs=(VMEM,) * len(out_shape),
    )(*operands)


def body(samples, beam_weights, subarrays, training):
    range_count = lax.axis_size("range")
    core_count = lax.axis_size("sub")
    parts_iq, chan_dev, all_gates, pulses = samples.shape
    devices = range_count * core_count
    gate_dev = all_gates // devices
    subs, _, size, half = beam_weights.shape[1:]
    beams = half * core_count
    channels = chan_dev * devices
    core = lax.axis_index("sub")
    single, half_type = jnp.float32, jnp.bfloat16
    shaped = jax.ShapeDtypeStruct

    rows = parts_iq * chan_dev * gate_dev
    chan_step = min(chan_dev, 8)
    spread = pl.pallas_call(
        spread_kernel,
        out_shape=shaped((devices, rows, pulses), single),
        grid=(chan_dev // chan_step,),
        in_specs=[pl.BlockSpec((parts_iq, chan_step, all_gates, pulses), lambda i: (0, i, 0, 0))],
        out_specs=VMEM,
    )(samples)
    turned = lax.all_to_all(spread, AXES, 0, 0, tiled=True)
    sent = lax.dynamic_index_in_dim(beam_weights, 1 - core, 0, keepdims=False)
    got = lax.ppermute(sent, "sub", [(0, 1), (1, 0)])
    hot, sub_weights, chan_weights = call(
        prepare_kernel,
        (
            shaped((channels, channels), half_type),
            shaped((2, channels, 2 * beams), half_type),
            shaped((2, channels, 2 * beams), half_type),
        ),
        [SMEM, VMEM, VMEM, VMEM],
        core.reshape(1).astype(jnp.int32),
        near(beam_weights),
        near(got),
        near(subarrays.reshape(subs * size, 1)),
    )
    snaps, outs, energies = call(
        beam_kernel,
        (
            shaped((2, channels, parts_iq * gate_dev * pulses), half_type),
            shaped((parts_iq, beams, gate_dev * pulses), single),
            shaped((devices, beams), single),
        ),
        [VMEM, VMEM],
        near(turned),
        chan_weights,
    )
    shared = lax.all_to_all(energies, AXES, 0, 0, tiled=True)
    covs, filts = call(
        functools.partial(covariance_kernel, factor=1.0 / (GB * pulses)),
        (
            shaped((1, subs, size, 2 * size), single),
            shaped((parts_iq, beams * gate_dev, pulses), single),
        ),
        [SMEM, VMEM, VMEM, VMEM, VMEM],
        training,
        hot,
        snaps,
        sub_weights,
        outs,
    )
    filtered = filts.reshape(parts_iq, beams, gate_dev, pulses)
    energy = jnp.sum(shared, axis=0) * (1.0 / (all_gates * pulses))
    return (covs, filtered, energy)


def solution(mesh):
    placed = (
        P(None, ("groups", "range", "sub"), None, None),
        P(("groups", "range"), None, None, None, "sub"),
        P(("groups", "range", "sub"), None, None),
        P(("groups", "range", "sub")),
    )
    return jax.shard_map(
        body,
        mesh=mesh,
        in_specs=placed,
        out_specs=(
            P(("groups", "range", "sub"), None, None, None),
            P(None, None, ("groups", "range", "sub"), None),
            P("groups"),
        ),
        check_vma=False,
    )
```

time: 55.8 us -> 51.1 us (0.916)
  blocking collectives: 13.2 us -> 0 us
  starting transfers between devices: 7.98 us -> 14.8 us
  Pallas kernels: 6.84 us -> 13.6 us
  local copies, waits for them, and re-layouts: 4.86 us -> 0.41 us
  waiting for transfers between devices: 21.3 us -> 20.7 us
    all_to_all x1 -> x0, blocking collectives: 13.2 us -> none  [body(): shared = lax.all_to_all(energies, AXES, 0, 0, tiled=True)]
    all_to_all x0 -> x1, starting transfers between devices: none -> 6.79 us  [body(): shared = lax.all_to_all(energies, AXES, 0, 0, tiled=True)]
    pallas_call x1 -> x4, Pallas kernels: 6.84 us -> 13.6 us  [the longest x3 10.2 us: call(): pl.pallas_call(kernel, out_shape=out_shape, in_specs=in_specs, out_specs=...]
    reshape x1 -> x0, local copies, waits for them, and re-layouts: 2.77 us -> none  [body(): samples.reshape(parts_iq, chan_dev, devices, gate_dev, pulses)]
    all_to_all x1, waiting for transfers between devices: 20.8 us -> 19.2 us  [body(): turned = lax.all_to_all(spread, AXES, 0, 0, tiled=True)]
    unnamed x8 -> x4, local copies, waits for them, and re-layouts: 1.14 us -> 0.17 us
    reshape x1, local copies, waits for them, and re-layouts: 0.9 us -> 0.2 us  [body(): subarrays.reshape(subs * size, 1)]
    ppermute x1, waiting for transfers between devices: 0.51 us -> 1.2 us  [body(): got = lax.ppermute(sent, 'sub', [(0, 1), (1, 0)])]
  transfers between devices with their start and end apart: 2 -> 3, of which waited for: 2 -> 3; matrix products, arithmetic and copies ran while one was open for 2% -> 0% of each run, Pallas kernels for 0% -> 15%
where the time goes in v2:
time: 51.1 us; the launch traced here: 50.7 us
  waiting for transfers between devices  20.7 us (41%)
  starting transfers between devices  14.8 us (29%)
  Pallas kernels  13.6 us (27%)
  between operations  0.69 us (1%)
  other arithmetic  0.55 us (1%)
    all_to_all x1, waiting for transfers between devices, body(): turned = lax.all_to_all(spread, AXES, 0, 0, tiled=True)  19.2 us
    pallas_call x3, Pallas kernels, call(): pl.pallas_call(kernel, out_shape=out_shape, in_specs=in_specs, out_specs=...  10.2 us
    all_to_all x1, starting transfers between devices, body(): turned = lax.all_to_all(spread, AXES, 0, 0, tiled=True)  7.52 us
    all_to_all x1, starting transfers between devices, body(): shared = lax.all_to_all(energies, AXES, 0, 0, tiled=True)  6.79 us
    pallas_call x1, Pallas kernels, body(): pl.pallas_call(spread_kernel, out_shape=shaped((devices, rows, pulses), s...  3.4 us
    ppermute x1, waiting for transfers between devices, body(): got = lax.ppermute(sent, 'sub', [(0, 1), (1, 0)])  1.2 us
  transfers between devices with their start and end apart: 3, of which 3 were waited for; matrix products, arithmetic and copies ran while one was open for 0% of the time, Pallas kernels for 15%

profile of v2, /device:TPU:0, one launch (start us, length us, event | category | flops | bytes accessed | tf_op | source)
XLA Modules:
  0.0 50.7 jit_solution(17964304895196424463)
XLA Ops:
  0.6 3.4 %shard_map.68 = f32[16,128,128]{2,1,0:T(8,128)} custom-call(f32[2,32,32,128]{3,2,1,0:T(8,128)} %samples.1), custom_call_target="tpu_custom_call" | custom-call | tf_op jit(solution)/shard_map/pallas_call | solution.py:159
  4.0 0.0 copy-start
  4.0 7.5 %all-to-all-start = ((f32[16,128,128]{2,1,0:T(8,128)}), f32[16,128,128]{2,1,0:T(8,128)S(1)}, u32[]{:S(2)}, u32[]{:S(2)}) async-start(f32[16,128,128]{2,1,0:T(8,128)} %shard_map.68), calls=%async_computation | async-start | bytes 2097152 | tf_op jit(solution)/shard_map/all_to_all | solution.py:166
  11.6 0.0 copy-done
  11.6 0.0 copy-start.1
  11.6 0.5 collective-permute-start
  12.1 0.2 copy-done.1
  12.3 0.2 reshape.20.chosen
  12.5 1.2 %collective-permute-done.got = f32[8,2,64,64]{3,2,1,0:T(8,128)S(1)} collective-permute-done((f32[8,2,64,64]{3,2,1,0:T(8,128)S(1)}, f32[8,2,64,64]{3,2,1,0:T(8,128)S(1)}, u32[]{:S(2)}, u32[]{:S(2)}) %collective-permute-start) | collective-permute-done | bytes 262176 | tf_op jit(solution)/shard_map/ppermute | solution.py:168
  13.7 1.6 %shard_map.67 = (bf16[512,512]{1,0:T(8,128)(2,1)}, bf16[2,512,256]{2,1,0:T(8,128)(2,1)}, bf16[2,512,256]{2,1,0:T(8,128)(2,1)}) custom-call(s32[1]{0:T(128)} %bitcast.core, f32[2,8,2,64,64]{4,3,2,1,0:T(8,128)S(1)} %copy-done, f32[8,2,64,64]{3,2,1,0:T(8,128)S(1)} %collective-permute-done.got, s32[512,1]{1,0:T(8,128)S(1)} %reshape.20.chosen), custom_call_target="tpu_custom_call" | custom-call | tf_op jit(solution)/shard_map/pallas_call | solution.py:136
  15.3 19.2 %all-to-all-done.turned = f32[16,128,128]{2,1,0:T(8,128)S(1)} async-done(((f32[16,128,128]{2,1,0:T(8,128)}), f32[16,128,128]{2,1,0:T(8,128)S(1)}, u32[]{:S(2)}, u32[]{:S(2)}) %all-to-all-start) | async-done | bytes 1048608 | tf_op jit(solution)/shard_map/all_to_all | solution.py:166
  34.4 2.5 %shard_map.69 = (bf16[2,512,512]{2,1,0:T(8,128)(2,1)}, f32[2,128,256]{2,1,0:T(8,128)}, f32[16,128]{1,0:T(8,128)}) custom-call(f32[16,128,128]{2,1,0:T(8,128)S(1)} %all-to-all-done.turned, bf16[2,512,256]{2,1,0:T(8,128)(2,1)} %get-tuple-element.12.weights), custom_call_target="tpu_custom_call" | custom-call | tf_op jit(solution)/shard_map/pallas_call | solution.py:136
  36.9 6.8 %all-to-all-start.1 = ((f32[16,1,128]{2,1,0:T(1,128)}), f32[16,1,128]{2,1,0:T(1,128)S(1)}, u32[]{:S(2)}, u32[]{:S(2)}) async-start(f32[16,1,128]{2,1,0:T(1,128)} %bitcast.7), calls=%async_computation.1 | async-start | bytes 16384 | tf_op jit(solution)/shard_map/all_to_all | solution.py:193
  43.7 6.1 %shard_map.70 = (f32[1,8,64,128]{3,2,1,0:T(8,128)}, f32[2,256,128]{2,1,0:T(8,128)}) custom-call(s32[2]{0:T(128)} %gates.1, bf16[512,512]{1,0:T(8,128)(2,1)} %get-tuple-element.11.hot, bf16[2,512,512]{2,1,0:T(8,128)(2,1)} %get-tuple-element.13.snaps, bf16[2,512,256]{2,1,0:T(8,128)(2,1)} %get-tuple-element.14.weights, f32[2,128,256]{2,1,0:T(8,128)} %get-tuple-element.15.beam_in), custom_call_target="tpu_custom_call" | custom-call | tf_op jit(solution)/shard_map/pallas_call | solution.py:136
  49.8 0.4 all-to-all-done.1
  50.2 0.5 %broadcast_multiply_fusion = f32[128]{0:T(128)} fusion(f32[128]{0:T(128)S(1)} %reduce_sum.9), kind=kLoop, calls=%fused_computation.1 | loop fusion | flops 128 | bytes 1024 | tf_op jit(solution)/shard_map/mul | solution.py:208
  (2 shorter events, 0.1 us)
Async XLA Ops:
  4.0 7.5 %copy-start = (f32[2,8,2,64,64]{4,3,2,1,0:T(8,128)S(1)}, f32[2,8,2,64,64]{4,3,2,1,0:T(8,128)}, u32[]{:S(2)}) copy-start(f32[2,8,2,64,64]{4,3,2,1,0:T(8,128)} %own.1) | copy-start | bytes 1572868
  4.0 30.4 %all-to-all-start = ((f32[16,128,128]{2,1,0:T(8,128)}), f32[16,128,128]{2,1,0:T(8,128)S(1)}, u32[]{:S(2)}, u32[]{:S(2)}) async-start(f32[16,128,128]{2,1,0:T(8,128)} %shard_map.68), calls=%async_computation | async-start | bytes 2097152 | tf_op jit(solution)/shard_map/all_to_all | solution.py:166
  11.6 0.7 %copy-start.1 = (s32[1,8,64]{2,1,0:T(8,128)S(1)}, s32[1,8,64]{2,1,0:T(8,128)}, u32[]{:S(2)}) copy-start(s32[1,8,64]{2,1,0:T(8,128)} %param.6) | copy-start | bytes 6148
  11.6 2.0 %collective-permute-start = (f32[8,2,64,64]{3,2,1,0:T(8,128)S(1)}, f32[8,2,64,64]{3,2,1,0:T(8,128)S(1)}, u32[]{:S(2)}, u32[]{:S(2)}) collective-permute-start(f32[8,2,64,64]{3,2,1,0:T(8,128)S(1)} %dynamic-slice_bitcast_fusion), channel_id=1, source_target_pairs={{0,1},{1,0},{2,3},{3,2},{4,5},{5,4},{6,7},{7,6},{8,9},{9,8},{10,11... | collective-permute-start | bytes 786440 | tf_op jit(solution)/shard_map/ppermute | solution.py:168
  36.9 13.2 %all-to-all-start.1 = ((f32[16,1,128]{2,1,0:T(1,128)}), f32[16,1,128]{2,1,0:T(1,128)S(1)}, u32[]{:S(2)}, u32[]{:S(2)}) async-start(f32[16,1,128]{2,1,0:T(1,128)} %bitcast.7), calls=%async_computation.1 | async-start | bytes 16384 | tf_op jit(solution)/shard_map/all_to_all | solution.py:193

commit v3 on v2

--- a/solution.py
+++ b/solution.py
@@ -36,17 +36,22 @@
 
 def spread_kernel(samples, spread):
     parts_iq, chan_step, all_gates, pulses = samples.shape
-    devices, rows, _ = spread.shape
-    chan_dev = rows // (parts_iq * GB)
     flat = samples.reshape(parts_iq * chan_step * all_gates, pulses)
-    start = pl.multiple_of(pl.program_id(0) * chan_step, chan_step)
     for iq in range(parts_iq):
         for gate in range(all_gates):
             dest, inner = divmod(gate, GB)
             row = iq * chan_step * all_gates + gate
-            spread[dest, pl.ds((iq * GB + inner) * chan_dev + start, chan_step), :] = flat[
-                pl.ds(row, chan_step, stride=all_gates), :
-            ]
+            spread[dest, iq * GB + inner] = flat[pl.ds(row, chan_step, stride=all_gates), :]
+
+
+def snapshots(turned):
+    sources, rows, pulses = turned.shape
+    chan_dev = rows // (2 * GB)
+    columns = [
+        turned[:, piece * chan_dev:(piece + 1) * chan_dev, :].reshape(sources * chan_dev, pulses)
+        for piece in range(2 * GB)
+    ]
+    return split(jnp.concatenate(columns, axis=1))
 
 
 def prepare_kernel(core, own, got, chosen, hot_out, sub_out, chan_out):
@@ -66,18 +71,11 @@
         chan_out[index] = dot(hot, piece, OVER_ROWS).astype(jnp.bfloat16)
 
 
-def beam_kernel(turned, weights, snap_out, beam_out, energy_out):
-    sources, rows, pulses = turned.shape
-    chan_dev = rows // (2 * GB)
+def beam_kernel(turned, weights, beam_out, energy_out):
+    pulses = turned.shape[2]
     beams = weights.shape[2] // 2
     width = GB * pulses
-    columns = [
-        turned[:, piece * chan_dev:(piece + 1) * chan_dev, :].reshape(sources * chan_dev, pulses)
-        for piece in range(2 * GB)
-    ]
-    snaps = split(jnp.concatenate(columns, axis=1))
-    for index, piece in enumerate(snaps):
-        snap_out[index] = piece
+    snaps = snapshots(turned)
     mixed = dot3((weights[0], weights[1]), snaps, OVER_ROWS)
     out_real = mixed[:beams, :width] + mixed[beams:, width:]
     out_imag = mixed[:beams, width:] - mixed[beams:, :width]
@@ -91,12 +89,12 @@
     energy_out[...] = jnp.broadcast_to(total, energy_out.shape)
 
 
-def covariance_kernel(gates, hot, snaps, weights, beam_in, cov_out, filt_out, *, factor):
+def covariance_kernel(gates, hot, turned, weights, beam_in, cov_out, filt_out, *, factor):
     subs, size = cov_out.shape[1:3]
     beams = weights.shape[2] // 2
     width = beam_in.shape[2]
     pulses = width // GB
-    picked = [dot(hot[...], snaps[index], OVER_COLS_ROWS).astype(jnp.bfloat16) for index in range(2)]
+    picked = [dot(hot[...], piece, OVER_COLS_ROWS).astype(jnp.bfloat16) for piece in snapshots(turned)]
     column_gate = lax.broadcasted_iota(jnp.int32, (1, 2 * width), 1) // pulses % GB
     mask = jnp.zeros((1, 2 * width), jnp.float32)
     for gate in range(GB):
@@ -158,12 +156,12 @@
     chan_step = min(chan_dev, 8)
     spread = pl.pallas_call(
         spread_kernel,
-        out_shape=shaped((devices, rows, pulses), single),
+        out_shape=shaped((devices, parts_iq * gate_dev, chan_dev, pulses), single),
         grid=(chan_dev // chan_step,),
         in_specs=[pl.BlockSpec((parts_iq, chan_step, all_gates, pulses), lambda i: (0, i, 0, 0))],
-        out_specs=VMEM,
-    )(samples)
-    turned = lax.all_to_all(spread, AXES, 0, 0, tiled=True)
+        out_specs=pl.BlockSpec((devices, parts_iq * gate_dev, chan_step, pulses), lambda i: (0, 0, i, 0)),
+    )(samples).reshape(devices, rows, pulses)
+    turned = near(lax.all_to_all(spread, AXES, 0, 0, tiled=True))
     sent = lax.dynamic_index_in_dim(beam_weights, 1 - core, 0, keepdims=False)
     got = lax.ppermute(sent, "sub", [(0, 1), (1, 0)])
     hot, sub_weights, chan_weights = call(
@@ -179,16 +177,15 @@
         near(got),
         near(subarrays.reshape(subs * size, 1)),
     )
-    snaps, outs, energies = call(
+    outs, energies = call(
         beam_kernel,
         (
-            shaped((2, channels, parts_iq * gate_dev * pulses), half_type),
             shaped((parts_iq, beams, gate_dev * pulses), single),
             shaped((devices, beams), single),
         ),
         [VMEM, VMEM],
-        near(turned),
-        chan_weights,
+        turned,
+        near(chan_weights),
     )
     shared = lax.all_to_all(energies, AXES, 0, 0, tiled=True)
     covs, filts = call(
@@ -199,9 +196,9 @@
         ),
         [SMEM, VMEM, VMEM, VMEM, VMEM],
         training,
-        hot,
-        snaps,
-        sub_weights,
+        near(hot),
+        turned,
+        near(sub_weights),
         outs,
     )
     filtered = filts.reshape(parts_iq, beams, gate_dev, pulses)

time: 51.1 us -> 51.3 us (level)
  Pallas kernels: 13.6 us -> 12.1 us
  local copies, waits for them, and re-layouts: 0.41 us -> 1.46 us
  waiting for transfers between devices: 20.7 us -> 21.3 us
    pallas_call x3, Pallas kernels: 10.2 us -> 8.4 us  [call(): pl.pallas_call(kernel, out_shape=out_shape, in_specs=in_specs, out_specs=...]
    unnamed x4 -> x10, local copies, waits for them, and re-layouts: 0.17 us -> 1.21 us
    all_to_all x1, waiting for transfers between devices: 0.36 us -> 0.96 us  [body(): shared = lax.all_to_all(energies, AXES, 0, 0, tiled=True)]
  transfers between devices with their start and end apart: 3 -> 3, of which waited for: 3 -> 3; matrix products, arithmetic and copies ran while one was open for 0% -> 0% of each run, Pallas kernels for 15% -> 14%
where the time goes in v3:
time: 51.3 us; the launch traced here: 50.9 us
  waiting for transfers between devices  21.3 us (42%)
  starting transfers between devices  14.8 us (29%)
  Pallas kernels  12.1 us (24%)
  local copies, waits for them, and re-layouts  1.46 us (3%)
  between operations  0.71 us (1%)
  other arithmetic  0.55 us (1%)
    all_to_all x1, waiting for transfers between devices, body(): turned = near(lax.all_to_all(spread, AXES, 0, 0, tiled=True))  19.2 us
    pallas_call x3, Pallas kernels, call(): pl.pallas_call(kernel, out_shape=out_shape, in_specs=in_specs, out_specs=...  8.4 us
    all_to_all x1, starting transfers between devices, body(): turned = near(lax.all_to_all(spread, AXES, 0, 0, tiled=True))  7.52 us
    all_to_all x1, starting transfers between devices, body(): shared = lax.all_to_all(energies, AXES, 0, 0, tiled=True)  6.79 us
    pallas_call x1, Pallas kernels, body(): pl.pallas_call(spread_kernel, out_shape=shaped((devices, parts_iq * gate_...  3.69 us
    unnamed x10, local copies, waits for them, and re-layouts  1.21 us
    ppermute x1, waiting for transfers between devices, body(): got = lax.ppermute(sent, 'sub', [(0, 1), (1, 0)])  1.2 us
  transfers between devices with their start and end apart: 3, of which 3 were waited for; matrix products, arithmetic and copies ran while one was open for 0% of the time, Pallas kernels for 14%

profile of v3, /device:TPU:0, one launch (start us, length us, event | category | flops | bytes accessed | tf_op | source)
XLA Modules:
  0.0 50.9 jit_solution(6507667936585129139)
XLA Ops:
  0.6 3.7 %shard_map.68 = f32[16,4,32,128]{3,2,1,0:T(8,128)} custom-call(f32[2,32,32,128]{3,2,1,0:T(8,128)} %samples.1), custom_call_target="tpu_custom_call" | custom-call | tf_op jit(solution)/shard_map/pallas_call | solution.py:157
  4.3 0.0 copy-start
  4.3 7.5 %all-to-all-start = ((f32[16,128,128]{2,1,0:T(8,128)}), f32[16,128,128]{2,1,0:T(8,128)S(1)}, u32[]{:S(2)}, u32[]{:S(2)}) async-start(f32[16,128,128]{2,1,0:T(8,128)} %bitcast.8), calls=%async_computation | async-start | bytes 2097152 | tf_op jit(solution)/shard_map/all_to_all | solution.py:164
  11.8 0.0 copy-done
  11.9 0.0 copy-start.4
  11.9 0.5 collective-permute-start
  12.4 0.2 copy-done.4
  12.6 0.2 reshape.24.chosen
  12.8 1.2 %collective-permute-done.got = f32[8,2,64,64]{3,2,1,0:T(8,128)S(1)} collective-permute-done((f32[8,2,64,64]{3,2,1,0:T(8,128)S(1)}, f32[8,2,64,64]{3,2,1,0:T(8,128)S(1)}, u32[]{:S(2)}, u32[]{:S(2)}) %collective-permute-start) | collective-permute-done | bytes 262176 | tf_op jit(solution)/shard_map/ppermute | solution.py:166
  14.0 1.6 %shard_map.67 = (bf16[512,512]{1,0:T(8,128)(2,1)}, bf16[2,512,256]{2,1,0:T(8,128)(2,1)}, bf16[2,512,256]{2,1,0:T(8,128)(2,1)}) custom-call(s32[1]{0:T(128)} %bitcast.core, f32[2,8,2,64,64]{4,3,2,1,0:T(8,128)S(1)} %copy-done, f32[8,2,64,64]{3,2,1,0:T(8,128)S(1)} %collective-permute-done.got, s32[512,1]{1,0:T(8,128)S(1)} %reshape.24.chosen), custom_call_target="tpu_custom_call" | custom-call | tf_op jit(solution)/shard_map/pallas_call | solution.py:134
  15.6 19.2 %all-to-all-done.turned = f32[16,128,128]{2,1,0:T(8,128)S(1)} async-done(((f32[16,128,128]{2,1,0:T(8,128)}), f32[16,128,128]{2,1,0:T(8,128)S(1)}, u32[]{:S(2)}, u32[]{:S(2)}) %all-to-all-start) | async-done | bytes 1048608 | tf_op jit(solution)/shard_map/all_to_all | solution.py:164
  34.7 0.0 copy-start.3
  34.7 1.0 %copy-done.3 = bf16[2,512,256]{2,1,0:T(8,128)(2,1)S(1)} copy-done((bf16[2,512,256]{2,1,0:T(8,128)(2,1)S(1)}, bf16[2,512,256]{2,1,0:T(8,128)(2,1)}, u32[]{:S(2)}) %copy-start.3) | copy-done | bytes 524312
  35.8 0.0 copy-start.1
  35.8 0.0 copy-start.2
  35.8 1.3 %shard_map.69 = (f32[2,128,256]{2,1,0:T(8,128)}, f32[16,128]{1,0:T(8,128)}) custom-call(f32[16,128,128]{2,1,0:T(8,128)S(1)} %all-to-all-done.turned, bf16[2,512,256]{2,1,0:T(8,128)(2,1)S(1)} %copy-done.3), custom_call_target="tpu_custom_call" | custom-call | tf_op jit(solution)/shard_map/pallas_call | solution.py:134
  37.1 6.8 %all-to-all-start.1 = ((f32[16,1,128]{2,1,0:T(1,128)}), f32[16,1,128]{2,1,0:T(1,128)S(1)}, u32[]{:S(2)}, u32[]{:S(2)}) async-start(f32[16,1,128]{2,1,0:T(1,128)} %bitcast.9), calls=%async_computation.1 | async-start | bytes 16384 | tf_op jit(solution)/shard_map/all_to_all | solution.py:190
  43.9 0.0 copy-done.1
  43.9 0.0 copy-done.2
  43.9 5.5 %shard_map.70 = (f32[1,8,64,128]{3,2,1,0:T(8,128)}, f32[2,256,128]{2,1,0:T(8,128)}) custom-call(s32[2]{0:T(128)} %gates.1, bf16[512,512]{1,0:T(8,128)(2,1)S(1)} %copy-done.1, f32[16,128,128]{2,1,0:T(8,128)S(1)} %all-to-all-done.turned, bf16[2,512,256]{2,1,0:T(8,128)(2,1)S(1)} %copy-done.2, f32[2,128,256]{2,1,0:T(8,128)} %get-tuple-element.13.beam_in), custom_call_target="tpu_custom_call" | custom-call | tf_op jit(solution)/shard_map/pallas_call | solution.py:134
  49.4 1.0 %all-to-all-done.1 = f32[16,1,128]{2,1,0:T(1,128)S(1)} async-done(((f32[16,1,128]{2,1,0:T(1,128)}), f32[16,1,128]{2,1,0:T(1,128)S(1)}, u32[]{:S(2)}, u32[]{:S(2)}) %all-to-all-start.1) | async-done | bytes 8224 | tf_op jit(solution)/shard_map/all_to_all | solution.py:190
  50.4 0.5 %broadcast_multiply_fusion = f32[128]{0:T(128)} fusion(f32[128]{0:T(128)S(1)} %reduce_sum.9), kind=kLoop, calls=%fused_computation.1 | loop fusion | flops 128 | bytes 1024 | tf_op jit(solution)/shard_map/mul | solution.py:205
  (2 shorter events, 0.1 us)
Async XLA Ops:
  4.3 7.5 %copy-start = (f32[2,8,2,64,64]{4,3,2,1,0:T(8,128)S(1)}, f32[2,8,2,64,64]{4,3,2,1,0:T(8,128)}, u32[]{:S(2)}) copy-start(f32[2,8,2,64,64]{4,3,2,1,0:T(8,128)} %own.1) | copy-start | bytes 1572868
  4.3 30.4 %all-to-all-start = ((f32[16,128,128]{2,1,0:T(8,128)}), f32[16,128,128]{2,1,0:T(8,128)S(1)}, u32[]{:S(2)}, u32[]{:S(2)}) async-start(f32[16,128,128]{2,1,0:T(8,128)} %bitcast.8), calls=%async_computation | async-start | bytes 2097152 | tf_op jit(solution)/shard_map/all_to_all | solution.py:164
  11.9 0.7 %copy-start.4 = (s32[1,8,64]{2,1,0:T(8,128)S(1)}, s32[1,8,64]{2,1,0:T(8,128)}, u32[]{:S(2)}) copy-start(s32[1,8,64]{2,1,0:T(8,128)} %param.6) | copy-start | bytes 6148
  11.9 2.0 %collective-permute-start = (f32[8,2,64,64]{3,2,1,0:T(8,128)S(1)}, f32[8,2,64,64]{3,2,1,0:T(8,128)S(1)}, u32[]{:S(2)}, u32[]{:S(2)}) collective-permute-start(f32[8,2,64,64]{3,2,1,0:T(8,128)S(1)} %dynamic-slice_bitcast_fusion), channel_id=1, source_target_pairs={{0,1},{1,0},{2,3},{3,2},{4,5},{5,4},{6,7},{7,6},{8,9},{9,8},{10,11... | collective-permute-start | bytes 786440 | tf_op jit(solution)/shard_map/ppermute | solution.py:166
  34.7 1.0 %copy-start.3 = (bf16[2,512,256]{2,1,0:T(8,128)(2,1)S(1)}, bf16[2,512,256]{2,1,0:T(8,128)(2,1)}, u32[]{:S(2)}) copy-start(bf16[2,512,256]{2,1,0:T(8,128)(2,1)} %get-tuple-element.12.weights) | copy-start | bytes 1572868
  35.8 8.1 %copy-start.1 = (bf16[512,512]{1,0:T(8,128)(2,1)S(1)}, bf16[512,512]{1,0:T(8,128)(2,1)}, u32[]{:S(2)}) copy-start(bf16[512,512]{1,0:T(8,128)(2,1)} %get-tuple-element.10.hot) | copy-start | bytes 1572868
  35.8 8.1 %copy-start.2 = (bf16[2,512,256]{2,1,0:T(8,128)(2,1)S(1)}, bf16[2,512,256]{2,1,0:T(8,128)(2,1)}, u32[]{:S(2)}) copy-start(bf16[2,512,256]{2,1,0:T(8,128)(2,1)} %get-tuple-element.11.weights) | copy-start | bytes 1572868
  37.1 13.2 %all-to-all-start.1 = ((f32[16,1,128]{2,1,0:T(1,128)}), f32[16,1,128]{2,1,0:T(1,128)S(1)}, u32[]{:S(2)}, u32[]{:S(2)}) async-start(f32[16,1,128]{2,1,0:T(1,128)} %bitcast.9), calls=%async_computation.1 | async-start | bytes 16384 | tf_op jit(solution)/shard_map/all_to_all | solution.py:190

commit v4 on v3

--- a/solution.py
+++ b/solution.py
@@ -34,23 +34,16 @@
     return dot(lh, rh, dims) + (dot(lh, rl, dims) + dot(ll, rh, dims))
 
 
-def spread_kernel(samples, spread):
-    parts_iq, chan_step, all_gates, pulses = samples.shape
-    flat = samples.reshape(parts_iq * chan_step * all_gates, pulses)
-    for iq in range(parts_iq):
-        for gate in range(all_gates):
-            dest, inner = divmod(gate, GB)
-            row = iq * chan_step * all_gates + gate
-            spread[dest, iq * GB + inner] = flat[pl.ds(row, chan_step, stride=all_gates), :]
-
-
 def snapshots(turned):
     sources, rows, pulses = turned.shape
     chan_dev = rows // (2 * GB)
-    columns = [
-        turned[:, piece * chan_dev:(piece + 1) * chan_dev, :].reshape(sources * chan_dev, pulses)
-        for piece in range(2 * GB)
-    ]
+    flat = turned.reshape(sources * rows, pulses)
+    columns = []
+    for iq in range(2):
+        for gate in range(GB):
+            starts = [src * rows + iq * chan_dev * GB + gate for src in range(sources)]
+            pieces = [flat[pl.ds(start, chan_dev, stride=GB), :] for start in starts]
+            columns.append(jnp.concatenate(pieces, axis=0))
     return split(jnp.concatenate(columns, axis=1))
 
 
@@ -153,14 +146,8 @@
     shaped = jax.ShapeDtypeStruct
 
     rows = parts_iq * chan_dev * gate_dev
-    chan_step = min(chan_dev, 8)
-    spread = pl.pallas_call(
-        spread_kernel,
-        out_shape=shaped((devices, parts_iq * gate_dev, chan_dev, pulses), single),
-        grid=(chan_dev // chan_step,),
-        in_specs=[pl.BlockSpec((parts_iq, chan_step, all_gates, pulses), lambda i: (0, i, 0, 0))],
-        out_specs=pl.BlockSpec((devices, parts_iq * gate_dev, chan_step, pulses), lambda i: (0, 0, i, 0)),
-    )(samples).reshape(devices, rows, pulses)
+    spread = samples.reshape(parts_iq, chan_dev, devices, gate_dev, pulses).transpose(2, 0, 1, 3, 4)
+    spread = spread.reshape(devices, rows, pulses)
     turned = near(lax.all_to_all(spread, AXES, 0, 0, tiled=True))
     sent = lax.dynamic_index_in_dim(beam_weights, 1 - core, 0, keepdims=False)
     got = lax.ppermute(sent, "sub", [(0, 1), (1, 0)])
@@ -185,7 +172,7 @@
         ),
         [VMEM, VMEM],
         turned,
-        near(chan_weights),
+        chan_weights,
     )
     shared = lax.all_to_all(energies, AXES, 0, 0, tiled=True)
     covs, filts = call(

time: 51.3 us -> 50.4 us (0.982)
  Pallas kernels: 12.1 us -> 9.52 us
  local copies, waits for them, and re-layouts: 1.46 us -> 3.84 us
  waiting for transfers between devices: 21.3 us -> 20.7 us
    pallas_call x1 -> x0, Pallas kernels: 3.69 us -> none  [body(): pl.pallas_call(spread_kernel, out_shape=shaped((devices, parts_iq * gate_...]
    reshape x0 -> x1, local copies, waits for them, and re-layouts: none -> 2.76 us  [body(): samples.reshape(parts_iq, chan_dev, devices, gate_dev, pulses)]
    unnamed x10 -> x8, local copies, waits for them, and re-layouts: 1.21 us -> 0.02 us
    pallas_call x3, Pallas kernels: 8.4 us -> 9.52 us  [call(): pl.pallas_call(kernel, out_shape=out_shape, in_specs=in_specs, out_specs=...]
    all_to_all x1, waiting for transfers between devices: 19.2 us -> 18.2 us  [body(): turned = near(lax.all_to_all(spread, AXES, 0, 0, tiled=True))]
    squeeze x1, local copies, waits for them, and re-layouts: 0.05 us -> 0.86 us  [body(): sent = lax.dynamic_index_in_dim(beam_weights, 1 - core, 0, keepdims=False)]
  transfers between devices with their start and end apart: 3 -> 3, of which waited for: 3 -> 3; matrix products, arithmetic and copies ran while one was open for 0% -> 2% of each run, Pallas kernels for 14% -> 14%
where the time goes in v4:
time: 50.4 us; the launch traced here: 50.1 us
  waiting for transfers between devices  20.7 us (41%)
  starting transfers between devices  14.7 us (29%)
  Pallas kernels  9.52 us (19%)
  local copies, waits for them, and re-layouts  3.84 us (8%)
  between operations  0.7 us (1%)
  other arithmetic  0.55 us (1%)
    all_to_all x1, waiting for transfers between devices, body(): turned = near(lax.all_to_all(spread, AXES, 0, 0, tiled=True))  18.2 us
    pallas_call x3, Pallas kernels, call(): pl.pallas_call(kernel, out_shape=out_shape, in_specs=in_specs, out_specs=...  9.52 us
    all_to_all x1, starting transfers between devices, body(): turned = near(lax.all_to_all(spread, AXES, 0, 0, tiled=True))  7.52 us
    all_to_all x1, starting transfers between devices, body(): shared = lax.all_to_all(energies, AXES, 0, 0, tiled=True)  6.79 us
    reshape x1, local copies, waits for them, and re-layouts, body(): samples.reshape(parts_iq, chan_dev, devices, gate_dev, pulses)  2.76 us
    ppermute x1, waiting for transfers between devices, body(): got = lax.ppermute(sent, 'sub', [(0, 1), (1, 0)])  1.54 us
  transfers between devices with their start and end apart: 3, of which 3 were waited for; matrix products, arithmetic and copies ran while one was open for 2% of the time, Pallas kernels for 14%

profile of v4, /device:TPU:0, one launch (start us, length us, event | category | flops | bytes accessed | tf_op | source)
XLA Modules:
  0.0 50.1 jit_solution(11759114314176462120)
XLA Ops:
  0.6 2.8 %copy.11 = f32[2,32,16,2,128]{4,3,1,0,2:T(2,128)} copy(f32[2,32,16,2,128]{4,3,2,1,0:T(2,128)} %bitcast.11) | data formatting | bytes 2097152 | tf_op jit(solution)/shard_map/reshape | solution.py:149
  3.4 0.0 copy-start
  3.4 7.5 %all-to-all-start = ((f32[16,128,128]{2,1,0:T(8,128)}), f32[16,128,128]{2,1,0:T(8,128)S(1)}, u32[]{:S(2)}, u32[]{:S(2)}) async-start(f32[16,128,128]{2,1,0:T(8,128)} %bitcast.4), calls=%async_computation | async-start | bytes 2097152 | tf_op jit(solution)/shard_map/all_to_all | solution.py:151
  10.9 0.0 copy-done
  10.9 0.0 copy-start.3
  10.9 0.9 %dynamic-slice_bitcast_fusion = f32[8,2,64,64]{3,2,1,0:T(8,128)} fusion(f32[2,8,2,64,64]{4,3,2,1,0:T(8,128)S(1)} %copy-done, s32[]{:T(128)S(6)} %select_n.4), kind=kLoop, calls=%fused_computation | loop fusion | bytes 524292 | tf_op jit(solution)/shard_map/jit(dynamic_index_in_dim)/squeeze | solution.py:152
  11.8 0.4 collective-permute-start
  12.2 0.0 copy-done.3
  12.2 0.2 reshape.28.chosen
  12.4 1.5 %collective-permute-done.got = f32[8,2,64,64]{3,2,1,0:T(8,128)S(1)} collective-permute-done((f32[8,2,64,64]{3,2,1,0:T(8,128)}, f32[8,2,64,64]{3,2,1,0:T(8,128)S(1)}, u32[]{:S(2)}, u32[]{:S(2)}) %collective-permute-start) | collective-permute-done | bytes 262176 | tf_op jit(solution)/shard_map/ppermute | solution.py:153
  14.0 1.6 %shard_map.67 = (bf16[512,512]{1,0:T(8,128)(2,1)}, bf16[2,512,256]{2,1,0:T(8,128)(2,1)}, bf16[2,512,256]{2,1,0:T(8,128)(2,1)}) custom-call(s32[1]{0:T(128)} %bitcast.core, f32[2,8,2,64,64]{4,3,2,1,0:T(8,128)S(1)} %copy-done, f32[8,2,64,64]{3,2,1,0:T(8,128)S(1)} %collective-permute-done.got, s32[512,1]{1,0:T(8,128)S(1)} %reshape.28.chosen), custom_call_target="tpu_custom_call" | custom-call | tf_op jit(solution)/shard_map/pallas_call | solution.py:127
  15.6 18.2 %all-to-all-done.turned = f32[16,128,128]{2,1,0:T(8,128)S(1)} async-done(((f32[16,128,128]{2,1,0:T(8,128)}), f32[16,128,128]{2,1,0:T(8,128)S(1)}, u32[]{:S(2)}, u32[]{:S(2)}) %all-to-all-start) | async-done | bytes 1048608 | tf_op jit(solution)/shard_map/all_to_all | solution.py:151
  33.8 0.0 copy-start.1
  33.8 0.0 copy-start.2
  33.8 2.5 %shard_map.68 = (f32[2,128,256]{2,1,0:T(8,128)}, f32[16,128]{1,0:T(8,128)}) custom-call(f32[16,128,128]{2,1,0:T(8,128)S(1)} %all-to-all-done.turned, bf16[2,512,256]{2,1,0:T(8,128)(2,1)} %get-tuple-element.12.weights), custom_call_target="tpu_custom_call" | custom-call | tf_op jit(solution)/shard_map/pallas_call | solution.py:127
  36.3 6.8 %all-to-all-start.1 = ((f32[16,1,128]{2,1,0:T(1,128)}), f32[16,1,128]{2,1,0:T(1,128)S(1)}, u32[]{:S(2)}, u32[]{:S(2)}) async-start(f32[16,1,128]{2,1,0:T(1,128)} %bitcast.12), calls=%async_computation.1 | async-start | bytes 16384 | tf_op jit(solution)/shard_map/all_to_all | solution.py:177
  43.1 0.0 copy-done.1
  43.1 0.0 copy-done.2
  43.1 5.5 %shard_map.69 = (f32[1,8,64,128]{3,2,1,0:T(8,128)}, f32[2,256,128]{2,1,0:T(8,128)}) custom-call(s32[2]{0:T(128)} %gates.1, bf16[512,512]{1,0:T(8,128)(2,1)S(1)} %copy-done.1, f32[16,128,128]{2,1,0:T(8,128)S(1)} %all-to-all-done.turned, bf16[2,512,256]{2,1,0:T(8,128)(2,1)S(1)} %copy-done.2, f32[2,128,256]{2,1,0:T(8,128)} %get-tuple-element.13.beam_in), custom_call_target="tpu_custom_call" | custom-call | tf_op jit(solution)/shard_map/pallas_call | solution.py:127
  48.5 1.0 %all-to-all-done.1 = f32[16,1,128]{2,1,0:T(1,128)S(1)} async-done(((f32[16,1,128]{2,1,0:T(1,128)}), f32[16,1,128]{2,1,0:T(1,128)S(1)}, u32[]{:S(2)}, u32[]{:S(2)}) %all-to-all-start.1) | async-done | bytes 8224 | tf_op jit(solution)/shard_map/all_to_all | solution.py:177
  49.5 0.5 %broadcast_multiply_fusion = f32[128]{0:T(128)} fusion(f32[128]{0:T(128)S(1)} %reduce_sum.9), kind=kLoop, calls=%fused_computation.1 | loop fusion | flops 128 | bytes 1024 | tf_op jit(solution)/shard_map/mul | solution.py:192
  (1 shorter events, 0.0 us)
Async XLA Ops:
  3.4 7.5 %copy-start = (f32[2,8,2,64,64]{4,3,2,1,0:T(8,128)S(1)}, f32[2,8,2,64,64]{4,3,2,1,0:T(8,128)}, u32[]{:S(2)}) copy-start(f32[2,8,2,64,64]{4,3,2,1,0:T(8,128)} %own.1) | copy-start | bytes 1572868
  3.4 30.4 %all-to-all-start = ((f32[16,128,128]{2,1,0:T(8,128)}), f32[16,128,128]{2,1,0:T(8,128)S(1)}, u32[]{:S(2)}, u32[]{:S(2)}) async-start(f32[16,128,128]{2,1,0:T(8,128)} %bitcast.4), calls=%async_computation | async-start | bytes 2097152 | tf_op jit(solution)/shard_map/all_to_all | solution.py:151
  10.9 1.3 %copy-start.3 = (s32[1,8,64]{2,1,0:T(8,128)S(1)}, s32[1,8,64]{2,1,0:T(8,128)}, u32[]{:S(2)}) copy-start(s32[1,8,64]{2,1,0:T(8,128)} %param.6) | copy-start | bytes 6148
  11.8 2.1 %collective-permute-start = (f32[8,2,64,64]{3,2,1,0:T(8,128)}, f32[8,2,64,64]{3,2,1,0:T(8,128)S(1)}, u32[]{:S(2)}, u32[]{:S(2)}) collective-permute-start(f32[8,2,64,64]{3,2,1,0:T(8,128)} %dynamic-slice_bitcast_fusion), channel_id=1, source_target_pairs={{0,1},{1,0},{2,3},{3,2},{4,5},{5,4},{6,7},{7,6},{8,9},{9,8},{10,11... | collective-permute-start | bytes 786440 | tf_op jit(solution)/shard_map/ppermute | solution.py:153
  33.8 9.3 %copy-start.1 = (bf16[512,512]{1,0:T(8,128)(2,1)S(1)}, bf16[512,512]{1,0:T(8,128)(2,1)}, u32[]{:S(2)}) copy-start(bf16[512,512]{1,0:T(8,128)(2,1)} %get-tuple-element.10.hot) | copy-start | bytes 1572868
  33.8 9.3 %copy-start.2 = (bf16[2,512,256]{2,1,0:T(8,128)(2,1)S(1)}, bf16[2,512,256]{2,1,0:T(8,128)(2,1)}, u32[]{:S(2)}) copy-start(bf16[2,512,256]{2,1,0:T(8,128)(2,1)} %get-tuple-element.11.weights) | copy-start | bytes 1572868
  36.3 13.2 %all-to-all-start.1 = ((f32[16,1,128]{2,1,0:T(1,128)}), f32[16,1,128]{2,1,0:T(1,128)S(1)}, u32[]{:S(2)}, u32[]{:S(2)}) async-start(f32[16,1,128]{2,1,0:T(1,128)} %bitcast.12), calls=%async_computation.1 | async-start | bytes 16384 | tf_op jit(solution)/shard_map/all_to_all | solution.py:177
